TPU v7x, 16 devices: a whole 2x2x2 slice. The times are simulated.
16 devices in a mesh: proto: 4 (over z, y), data: 4 (over x, core).
Axes of the slice: x: 2, y: 2, z: 2, core: 2. Of those that a mesh axis runs over, the one named last changes fastest.
Arguments:
- emb_one: bfloat16 [8192, 256], P('data')
- emb_two: bfloat16 [8192, 256], P('data')
- protos: bfloat16 [1024, 256], P('proto')
Outputs:
- output 1: float32 [8192, 1024], P('data', 'proto')
- output 2: float32 [8192, 1024], P('data', 'proto')
- output 3: float32 [], replicated
- output 4: float32 [8192, 256], P('data')
- output 5: float32 [8192, 256], P('data')
- output 6: float32 [1024, 256], P('proto')
All inputs are finite; a program needn't handle non-finite values.
Results may differ from a plain program's by a relative error of at most 0.001.
Values are sent between devices in bfloat16 or wider.
A program may use at most 1 GiB of HBM per device.

v0:
```python
import jax
import jax.numpy as jnp
from jax import lax
from jax.sharding import PartitionSpec as P, NamedSharding

EPSILON = 0.05
TEMP_TAU = 0.1
value_a14 = 3


def solution(mesh):
    proto_size = mesh.shape['proto']
    data_size = mesh.shape['data']

    def local_step(emb_one, emb_two, protos):
        local_rows = emb_one.shape[0]
        total_rows = local_rows * data_size
        total_protos = protos.shape[0] * proto_size

        def view_terms(emb):
            scores = jnp.einsum('nd,kd->nk', emb, protos, preferred_element_type=jnp.float32)
            transport = jnp.exp(scores / EPSILON)
            for _ in range(value_a14):
                col_sum = lax.psum(jnp.sum(transport, axis=0), 'data')
                transport = transport / (total_protos * col_sum)
                row_sum = lax.psum(jnp.sum(transport, axis=1, keepdims=True), 'proto')
                transport = transport / (total_rows * row_sum)
            codes = total_rows * transport
            logits = scores / TEMP_TAU
            soft_denom = lax.psum(jnp.sum(jnp.exp(logits), axis=1, keepdims=True), 'proto')
            return codes, logits - jnp.log(soft_denom)

        codes_one, logp_one = view_terms(emb_one)
        codes_two, logp_two = view_terms(emb_two)
        part_loss = jnp.sum(codes_two * logp_one) + jnp.sum(codes_one * logp_two)
        loss_value = -lax.psum(part_loss, ('proto', 'data')) / (2 * total_rows)
        grad_scale = 2 * total_rows * TEMP_TAU
        logit_grad_one = ((jnp.exp(logp_one) - codes_two) / grad_scale).astype(jnp.bfloat16)
        logit_grad_two = ((jnp.exp(logp_two) - codes_one) / grad_scale).astype(jnp.bfloat16)
        grad_one = lax.psum(jnp.einsum('nk,kd->nd', logit_grad_one, protos, preferred_element_type=jnp.float32), 'proto')
        grad_two = lax.psum(jnp.einsum('nk,kd->nd', logit_grad_two, protos, preferred_element_type=jnp.float32), 'proto')
        proto_part = (jnp.einsum('nk,nd->kd', logit_grad_one, emb_one, preferred_element_type=jnp.float32)
                      + jnp.einsum('nk,nd->kd', logit_grad_two, emb_two, preferred_element_type=jnp.float32))
        grad_protos = lax.psum(proto_part, 'data')
        return codes_one, codes_two, loss_value, grad_one, grad_two, grad_protos

    return jax.shard_map(
        local_step, mesh=mesh,
        in_specs=(P('data', None), P('data', None), P('proto', None)),
        out_specs=(P('data', 'proto'), P('data', 'proto'), P(), P('data', None), P('data', None), P('proto', None)),
        check_vma=False)
```

profile of v0, /device:TPU:0, one launch (start us, length us, event | category | flops | bytes accessed | tf_op | source)
XLA Modules:
  0.0 274.8 jit_solution(4588540414012693901)
XLA Ops:
  7.2 0.0 copy-start
  7.2 0.0 all-reduce.7.cloned.1.call-start
  7.2 1.9 fusion.24
  9.1 8.6 %psum.126 = f32[256]{0:T(256)S(1)} all-reduce(f32[256]{0:T(256)S(1)} %get-tuple-element.36), channel_id=1, replica_groups=mesh['proto'=4,'data'=4] {'data'}, use_global_device_ids=true, to_apply=%region_1.0 | all-reduce | flops 256 | bytes 2048 | tf_op jit(solution)/shard_map/psum | solution.py:24
  17.7 0.7 exponential_reduce_fusion.1
  18.4 10.2 %psum.127 = f32[2048,1]{0,1:T(1,128)S(1)} all-reduce(f32[2048,1]{0,1:T(1,128)S(1)} %bitcast.52), channel_id=1, replica_groups=mesh['proto'=4,'data'=4] {'proto'}, use_global_device_ids=true, to_apply=%region_3.0 | all-reduce | flops 2048 | bytes 16384 | tf_op jit(solution)/shard_map/psum | solution.py:26
  28.6 0.6 fusion.16
  29.2 6.0 %psum.128 = f32[256]{0:T(256)S(1)} all-reduce(f32[256]{0:T(256)S(1)} %fusion.16), channel_id=1, replica_groups=mesh['proto'=4,'data'=4] {'data'}, use_global_device_ids=true, to_apply=%region_5.0 | all-reduce | flops 256 | bytes 2048 | tf_op jit(solution)/shard_map/psum | solution.py:24
  35.2 0.0 copy-start.9
  35.2 0.6 fusion.19
  35.8 7.9 %psum.129 = f32[2048,1]{0,1:T(1,128)S(1)} all-reduce(f32[2048,1]{0,1:T(1,128)S(1)} %bitcast.53), channel_id=1, replica_groups=mesh['proto'=4,'data'=4] {'proto'}, use_global_device_ids=true, to_apply=%region_7.0 | all-reduce | flops 2048 | bytes 16384 | tf_op jit(solution)/shard_map/psum | solution.py:26
  43.8 0.7 fusion.20
  44.5 0.0 copy-done
  44.5 0.0 copy-done.9
  44.5 2.1 exponential_reduce_fusion
  46.6 5.7 %all-reduce = (f32[256]{0:T(256)S(1)}, f32[256]{0:T(256)S(1)}) all-reduce(f32[256]{0:T(256)S(1)} %fusion.20, f32[256]{0:T(256)S(1)} %get-tuple-element.21), channel_id=1, replica_groups=mesh['proto'=4,'data'=4] {'data'}, use_global_device_ids=true, to_apply=%region_9.0 | all-reduce | flops 512 | bytes 4096 | tf_op jit(solution)/shard_map/psum | solution.py:24
  52.3 0.8 fusion.23
  53.1 15.3 %all-reduce.2 = (f32[2048,1]{0,1:T(1,128)S(1)}, f32[2048,1]{0,1:T(1,128)S(1)}) all-reduce(f32[2048,1]{0,1:T(1,128)S(1)} %bitcast.50, f32[2048,1]{0,1:T(1,128)S(1)} %bitcast.57), channel_id=1, replica_groups=mesh['proto'=4,'data'=4] {'proto'}, use_global_device_ids=true, to_apply=%region_11.0 | all-reduce | flops 4096 | bytes 32768 | tf_op jit(solution)/shard_map/psum | solution.py:26
  68.5 0.0 copy-start.1
  68.5 4.3 %multiply_convert_fusion = (bf16[2048,256]{0,1:T(8,128)(2,1)}, f32[2048,256]{0,1:T(8,128)S(1)}) fusion(f32[2048,256]{0,1:T(8,128)} %get-tuple-element.38, f32[2048]{0:T(1024)S(1)} %bitcast.46, f32[2048]{0:T(1024)S(1)} %bitcast.55, f32[256]{0:T(256)S(1)} %get-tuple-element.40, f32[2048]{0:T(1024)S(1)} %bitcast.40, f32[256]{0:T(256)S(1)} %broadcast_multiply_fusion.10, ...), kind=kLoop, calls=%fused_computation.20 | loop fusion | flops 6815744 | bytes 7375872 | tf_op jit(solution)/shard_map/convert_element_type | solution.py:39
  72.8 0.0 copy-start.2
  72.8 0.0 copy-done.1
  72.8 1.4 multiply_reduce_fusion
  74.2 0.0 copy-done.2
  74.2 7.8 %psum.133 = f32[2048,1]{0,1:T(1,128)S(1)} all-reduce(f32[2048,1]{0,1:T(1,128)S(1)} %bitcast.51), channel_id=1, replica_groups=mesh['proto'=4,'data'=4] {'proto'}, use_global_device_ids=true, to_apply=%region_15.0 | all-reduce | flops 2048 | bytes 16384 | tf_op jit(solution)/shard_map/psum | solution.py:26
  82.0 2.2 fusion.17
  84.2 5.8 %psum.134 = f32[256]{0:T(256)S(1)} all-reduce(f32[256]{0:T(256)S(1)} %fusion.17), channel_id=1, replica_groups=mesh['proto'=4,'data'=4] {'data'}, use_global_device_ids=true, to_apply=%region_17.0 | all-reduce | flops 256 | bytes 2048 | tf_op jit(solution)/shard_map/psum | solution.py:24
  90.0 2.2 fusion.18
  92.2 10.2 %psum.135 = f32[2048,1]{0,1:T(1,128)S(1)} all-reduce(f32[2048,1]{0,1:T(1,128)S(1)} %bitcast.54), channel_id=1, replica_groups=mesh['proto'=4,'data'=4] {'proto'}, use_global_device_ids=true, to_apply=%region_19.0 | all-reduce | flops 2048 | bytes 16384 | tf_op jit(solution)/shard_map/psum | solution.py:26
  102.4 2.3 fusion.21
  104.7 5.8 %psum.136 = f32[256]{0:T(256)S(1)} all-reduce(f32[256]{0:T(256)S(1)} %fusion.21), channel_id=1, replica_groups=mesh['proto'=4,'data'=4] {'data'}, use_global_device_ids=true, to_apply=%region_21.0 | all-reduce | flops 256 | bytes 2048 | tf_op jit(solution)/shard_map/psum | solution.py:24
  110.5 2.4 fusion.22
  112.9 13.9 %all-reduce.1 = (f32[2048,1]{0,1:T(1,128)S(1)}, f32[2048,1]{0,1:T(1,128)S(1)}) all-reduce(f32[2048,1]{0,1:T(1,128)S(1)} %bitcast.49, f32[2048,1]{0,1:T(1,128)S(1)} %bitcast.48), channel_id=1, replica_groups=mesh['proto'=4,'data'=4] {'proto'}, use_global_device_ids=true, to_apply=%region_23.0 | all-reduce | flops 4096 | bytes 32768 | tf_op jit(solution)/shard_map/psum | solution.py:26
  126.9 0.0 copy-start.7
  126.9 4.6 %multiply_convert_fusion.1 = (bf16[2048,256]{0,1:T(8,128)(2,1)S(1)}, f32[2048,256]{0,1:T(8,128)}) fusion(f32[2048,256]{0,1:T(8,128)S(1)} %get-tuple-element.37, f32[2048]{0:T(1024)S(1)} %bitcast.44, f32[2048]{0:T(1024)S(1)} %bitcast.56, f32[256]{0:T(256)S(1)} %broadcast_multiply_fusion.6, f32[2048]{0:T(1024)S(1)} %bitcast.43, ...), kind=kLoop, calls=%fused_computation.21 | loop fusion | flops 6815744 | bytes 7375872 | tf_op jit(solution)/shard_map/convert_element_type | solution.py:38
  131.5 0.0 copy-start.5
  131.5 0.0 copy-start.4
  131.5 1.0 copy-done.5
  132.4 0.0 copy-done.7
  132.4 0.4 fusion.30
  132.9 0.2 copy-done.4
  133.1 1.1 convolution_add_fusion
  134.2 0.0 all-reduce.7.cloned.1.call-update
  134.2 0.0 all-reduce.9.cloned.1.call-start
  134.3 0.0 copy-start.6
  134.3 3.1 %fusion.29 = f32[2048,256]{1,0:T(8,128)} fusion(bf16[2048,256]{0,1:T(8,128)(2,1)} %get-tuple-element.32, bf16[256,256]{1,0:T(8,128)(2,1)S(1)} %copy-done.9), kind=kOutput, calls=%fused_computation.54 | convolution fusion | flops 268435456 | bytes 3276800 | tf_op jit(solution)/shard_map/nk,kd->nd/dot_general | solution.py:41
  137.5 0.0 copy-done.6
  137.5 1.8 fusion.28
  139.3 0.0 all-reduce.9.cloned.1.call-update
  139.3 2.7 multiply_reduce_fusion.1
  143.3 31.3 %psum.140 = f32[]{:T(128)} all-reduce(f32[]{:T(128)S(6)} %add.42), channel_id=1, replica_groups=mesh['proto'=4,'data'=4] {'proto','data'}, use_global_device_ids=true, to_apply=%region_30.0 | all-reduce | flops 1 | bytes 8 | tf_op jit(solution)/shard_map/psum | solution.py:36
  174.7 0.0 copy-start.3
  174.7 3.0 %copy.11 = f32[2048,256]{1,0:T(8,128)} copy(f32[2048,256]{0,1:T(8,128)} %copy-done.2) | data formatting | bytes 4194304
  177.7 0.0 copy-done.3
  177.7 1.8 copy.12
  180.1 0.0 all-reduce.7.cloned.1.call-done
  180.2 81.4 %all-reduce.9.cloned.1.call-done = (f32[2048,256]{1,0:T(8,128)}, f32[2048,256]{1,0:T(8,128)}) async-done(((f32[2048,256]{1,0:T(8,128)}, f32[2048,256]{1,0:T(8,128)}), (f32[2048,256]{1,0:T(8,128)}, f32[2048,256]{1,0:T(8,128)})) %all-reduce.9.cloned.1.call-update) | async-done | bytes 4194320 | tf_op jit(solution)/shard_map/psum | solution.py:40
  261.6 0.0 copy-start.8
  261.6 3.2 %copy.16 = f32[2048,256]{1,0:T(8,128)} copy(f32[2048,256]{1,0:T(8,128)} %get-tuple-element.44) | data formatting | bytes 4194304
  264.8 0.0 copy-done.8
  264.8 0.0 copy-start.10
  264.8 1.3 copy.17
  266.1 0.0 copy-done.10
  266.1 0.7 copy.18
  (13 shorter events, 0.1 us)
Async XLA Ops:
  7.2 37.3 %copy-start = (bf16[2048,256]{1,0:T(8,128)(2,1)S(1)}, bf16[2048,256]{1,0:T(8,128)(2,1)}, u32[]{:S(2)}) copy-start(bf16[2048,256]{1,0:T(8,128)(2,1)} %param.4) | copy-start | bytes 3145732
  7.2 173.0 %all-reduce.7.cloned.1.call-start = ((), (), s32[]{:S(2)}) async-start(), calls=%async_computation | async-start | bytes 524288 | tf_op jit(solution)/shard_map/psum | solution.py:44
  35.2 9.3 %copy-start.9 = (bf16[256,256]{1,0:T(8,128)(2,1)S(1)}, bf16[256,256]{1,0:T(8,128)(2,1)}, u32[]{:S(2)}) copy-start(bf16[256,256]{1,0:T(8,128)(2,1)} %param.5) | copy-start | bytes 393220
  68.5 4.3 %copy-start.1 = (f32[2048,256]{0,1:T(8,128)S(1)}, f32[2048,256]{0,1:T(8,128)}, u32[]{:S(2)}) copy-start(f32[2048,256]{0,1:T(8,128)} %get-tuple-element.38) | copy-start | bytes 6291460
  72.8 1.4 copy-start.2
  126.9 5.5 %copy-start.7 = (bf16[2048,256]{1,0:T(8,128)(2,1)S(1)}, bf16[2048,256]{1,0:T(8,128)(2,1)}, u32[]{:S(2)}) copy-start(bf16[2048,256]{1,0:T(8,128)(2,1)} %param.3) | copy-start | bytes 3145732
  131.5 1.0 copy-start.5
  131.5 1.6 copy-start.4
  134.2 127.3 %all-reduce.9.cloned.1.call-start = ((), (), s32[]{:S(2)}) async-start(), calls=%async_computation.1 | async-start | bytes 8388608 | tf_op jit(solution)/shard_map/psum | solution.py:40
  134.3 3.2 %copy-start.6 = (bf16[2048,256]{0,1:T(8,128)(2,1)S(1)}, bf16[2048,256]{0,1:T(8,128)(2,1)}, u32[]{:S(2)}) copy-start(bf16[2048,256]{0,1:T(8,128)(2,1)} %copy-done.5) | copy-start | bytes 3145732
  174.7 3.0 %copy-start.3 = (f32[2048,256]{0,1:T(8,128)S(1)}, f32[2048,256]{0,1:T(8,128)}, u32[]{:S(2)}) copy-start(f32[2048,256]{0,1:T(8,128)} %get-tuple-element.35) | copy-start | bytes 6291460
  261.6 3.2 %copy-start.8 = (f32[2048,256]{1,0:T(8,128)S(1)}, f32[2048,256]{1,0:T(8,128)}, u32[]{:S(2)}) copy-start(f32[2048,256]{1,0:T(8,128)} %get-tuple-element.45) | copy-start | bytes 6291460
  264.8 1.3 copy-start.10
Sparse Core Ops, SparseCore 0:
  134.4 27.6 all-reduce.6
  165.5 96.0 all-reduce.8
where the time goes:
time: 275 us
  blocking collectives  129 us (47%)
  waiting for transfers between devices  81.5 us (30%)
  other arithmetic  25.6 us (9%)
  between operations  17.3 us (6%)
  local copies, waits for them, and re-layouts  11.3 us (4%)
  matrix products  10.5 us (4%)
    psum x1, waiting for transfers between devices, local_step(): lax.psum(jnp.einsum('nk,kd->nd', logit_grad_one, protos, preferred_elemen...  81.4 us
    psum x6, blocking collectives, view_terms(): row_sum = lax.psum(jnp.sum(transport, axis=1, keepdims=True), 'proto')  65.3 us
    psum x5, blocking collectives, view_terms(): col_sum = lax.psum(jnp.sum(transport, axis=0), 'data')  31.9 us
    psum x1, blocking collectives, local_step(): loss_value = -lax.psum(part_loss, ('proto', 'data')) / (2 * total_rows)  31.3 us
    unnamed x27, local copies, waits for them, and re-layouts  11.3 us
    reduce_sum x4, other arithmetic, view_terms(): row_sum = lax.psum(jnp.sum(transport, axis=1, keepdims=True), 'proto')  6 us
    reduce_sum x4, other arithmetic, view_terms(): col_sum = lax.psum(jnp.sum(transport, axis=0), 'data')  5.92 us
  transfers between devices with their start and end apart: 2, of which 1 were waited for; matrix products, arithmetic and copies ran while one was open for 5% of the time, Pallas kernels for 0%

commit v1 on v0

v1 whole, which is shorter than its diff:
```python
import functools
import math

import jax
import jax.numpy as jnp
from jax import lax
from jax.experimental import pallas as pl
from jax.experimental.pallas import tpu as pltpu
from jax.sharding import PartitionSpec as P

EPSILON = 0.05
TEMP_TAU = 0.1
ITERS = 3
MESH = pl.DeviceIdType.MESH
F32 = jnp.float32
LOG2E = math.log2(math.e)


def lanes(x):
    total = x[:, :128]
    for i in range(1, x.shape[1] // 128):
        total = total + x[:, i * 128:(i + 1) * 128]
    return total


def subl(x):
    return jnp.sum(x.reshape(x.shape[0] // 8, 8, x.shape[1]), axis=0)


def kernel(np_, nd, z1_ref, z2_ref, c_ref,
           code1, code2, loss_ref, g1, g2, gc,
           z, call, e, c1b, cb, dinv, h, hown, vb, dcp, dcr, dcs, lossb,
           lsem, csend, crecv, c1send, c1recv, bsend, brecv, dsend, drecv, lsend, lrecv):
    rows, kb = z.shape[1], call.shape[1]
    nrows, nk = rows * nd, kb * np_
    p, d = lax.axis_index("proto"), lax.axis_index("data")
    codes, grads = (code1, code2), (g1, g2)

    def remote(src, dst, ss, rs, pp, dd):
        return pltpu.make_async_remote_copy(src_ref=src, dst_ref=dst, send_sem=ss, recv_sem=rs,
                                            device_id={"proto": pp, "data": dd}, device_id_type=MESH)

    loads = [pltpu.make_async_copy(c_ref, call.at[p], lsem.at[0]),
             pltpu.make_async_copy(z1_ref, z.at[0], lsem.at[1]),
             pltpu.make_async_copy(z2_ref, z.at[1], lsem.at[2])]
    for cp in loads:
        cp.start()
    others = [(i, j) for i in range(np_) for j in range(nd) if i or j]
    barrier = pltpu.get_barrier_semaphore()
    for i, j in others:
        pl.semaphore_signal(barrier, inc=1, device_id={"proto": (p + i) % np_, "data": (d + j) % nd},
                            device_id_type=MESH)
    loads[0].wait()
    pl.semaphore_wait(barrier, len(others))

    gathers = []
    for q in range(1, np_):
        cp = remote(call.at[p], call.at[p], csend.at[q], crecv.at[q], (p + q) % np_, d)
        cp.start()
        gathers.append(cp)

    def scores(v, b, r):
        return lax.dot_general(z[v, r, :], call[b], (((1,), (1,)), ((), ())), preferred_element_type=F32)

    def chunk(i, size):
        return pl.ds(pl.multiple_of(i * size, size), size)

    RC = 256

    def exp_block(v, b, total):
        def body(i, acc):
            r = chunk(i, RC)
            x = jnp.exp2(scores(v, b, r) * (LOG2E / TEMP_TAU))
            e[v, b, r, :] = x
            return acc + subl(x * x) if total else acc
        return lax.fori_loop(0, rows // RC, body, jnp.zeros((8, kb), F32))

    own = []
    for v in range(2):
        loads[1 + v].wait()
        own.append(jnp.sum(exp_block(v, p, True), axis=0, keepdims=True))
    c1b[d * np_ + p] = jnp.concatenate(own, axis=0)
    firsts = []
    for n, (i, j) in enumerate(others):
        me = c1b.at[d * np_ + p]
        cp = remote(me, me, c1send.at[n], c1recv.at[n], (p + i) % np_, (d + j) % nd)
        cp.start()
        firsts.append(cp)

    for q in range(1, np_):
        gathers[q - 1].wait_recv()
        b = (p + np_ - q) % np_
        for v in range(2):
            exp_block(v, b, False)
    for cp in firsts:
        cp.wait_recv()
    for v in range(2):
        for b in range(np_):
            tot = c1b[b, v:v + 1, :]
            for j in range(1, nd):
                tot = tot + c1b[j * np_ + b, v:v + 1, :]
            vb[v, b] = jnp.broadcast_to(1.0 / (nk * tot), (8, kb))

    R2 = 64

    def scaled(v, b, r):
        x = e[v, b, r, :]
        n = r.size // 8
        return x, ((x * x).reshape(n, 8, kb) * vb[v, b][None]).reshape(n * 8, kb)

    def sweep(v, first):
        def body(i, accs):
            r = chunk(i, R2)
            racc = dacc = None
            for b in range(np_):
                x, t = scaled(v, b, r)
                t = lanes(t)
                racc = t if racc is None else racc + t
                if first:
                    s = lanes(x)
                    dacc = s if dacc is None else dacc + s
            u = 1.0 / (nrows * jnp.sum(racc, axis=1, keepdims=True))
            if first:
                dinv[v, r, :] = jnp.broadcast_to(jnp.sum(dacc, axis=1, keepdims=True), (R2, 128))
            out = []
            for b in range(np_):
                x = e[v, b, r, :]
                out.append(accs[b] + subl(x * x * u))
            return tuple(out)
        return lax.fori_loop(0, rows // R2, body, tuple(jnp.zeros((8, kb), F32) for _ in range(np_)))

    def exchange(it, v, accs):
        slot = (it * 2 + v) * nd
        for b in range(np_):
            cb[slot + d, :, b * kb:(b + 1) * kb] = jnp.sum(accs[b], axis=0, keepdims=True)
        out = []
        for q in range(1, nd):
            me = cb.at[slot + d]
            cp = remote(me, me, bsend.at[slot + q], brecv.at[slot + q], p, (d + q) % nd)
            cp.start()
            out.append(cp)
        return out

    def finish(it, v, copies):
        slot = (it * 2 + v) * nd
        for cp in copies:
            cp.wait_recv()
        tot = cb[slot]
        for j in range(1, nd):
            tot = tot + cb[slot + j]
        inv = 1.0 / (nk * tot)
        for b in range(np_):
            vb[v, b] = jnp.broadcast_to(inv[:, b * kb:(b + 1) * kb], (8, kb))

    pend, sends = [None, None], []
    for it in range(ITERS - 1):
        for v in range(2):
            if it:
                finish(it - 1, v, pend[v])
            pend[v] = exchange(it, v, sweep(v, it == 0))
            sends += pend[v]
    for v in range(2):
        finish(ITERS - 2, v, pend[v])

    R3 = 128
    scale = 1.0 / (2 * nrows * TEMP_TAU)

    def last(i, lacc):
        r = chunk(i, R3)
        rinv = []
        for v in range(2):
            racc = None
            for b in range(np_):
                t = lanes(scaled(v, b, r)[1])
                racc = t if racc is None else racc + t
            rinv.append(1.0 / jnp.sum(racc, axis=1, keepdims=True))
        den = [dinv[v, r, :] for v in range(2)]
        for v in range(2):
            w = 1 - v
            di = (scale / den[w])
            di = jnp.concatenate([di, di], axis=1)
            rs = rinv[v] * scale
            for b in range(np_):
                q = scaled(v, b, r)[1] * rs
                h[w, :, b * kb:(b + 1) * kb] = (e[w, b, r, :] * di - q).astype(jnp.bfloat16)
        for v in range(2):
            acc = None
            for b in range(np_):
                x = jnp.dot(h[v, :, b * kb:(b + 1) * kb], call[b], preferred_element_type=F32)
                acc = x if acc is None else acc + x
            grads[v][r, :] = acc
        for v in range(2):
            w = 1 - v
            x, t = scaled(v, p, r)
            q = t * rinv[v]
            codes[v][r, :] = q
            di = scale / den[w]
            di = jnp.concatenate([di, di], axis=1)
            hown[w, r, :] = (e[w, p, r, :] * di - t * (rinv[v] * scale)).astype(jnp.bfloat16)
            ld = jnp.log(den[w])
            logp = scores(w, p, r) * (1.0 / TEMP_TAU) - jnp.concatenate([ld, ld], axis=1)
            lacc = lacc + subl(lanes(q * logp))
        return lacc

    lacc = lax.fori_loop(0, rows // R3, last, jnp.zeros((8, 128), F32))
    dims = (((0,), (0,)), ((), ()))
    dcp[...] = (lax.dot_general(hown[0], z[0], dims, preferred_element_type=F32)
                + lax.dot_general(hown[1], z[1], dims, preferred_element_type=F32)).reshape(dcp.shape)
    core = d % 2
    mate, across = d + 1 - 2 * core, (d + 2) % nd
    s1 = remote(dcp.at[1 - core], dcr.at[0], dsend.at[0], drecv.at[0], p, mate)
    s1.start()
    lossb[d * np_ + p] = jnp.broadcast_to(jnp.sum(lacc).reshape(1, 1), (1, 128))
    lcopies = []
    for n, (i, j) in enumerate(others):
        me = lossb.at[d * np_ + p]
        cp = remote(me, me, lsend.at[n], lrecv.at[n], (p + i) % np_, (d + j) % nd)
        cp.start()
        lcopies.append(cp)
    s1.wait_recv()
    dcs[...] = dcp[core] + dcr[0]
    s2 = remote(dcs, dcr.at[1], dsend.at[1], drecv.at[1], p, across)
    s2.start()
    for cp in lcopies:
        cp.wait_recv()
    tot = lossb[0]
    for n in range(1, np_ * nd):
        tot = tot + lossb[n]
    loss_ref[0, 0] = jnp.sum(tot[:, :1]) * (-1.0 / (2 * nrows))
    s2.wait_recv()
    half = kb // 2
    mine = gc.at[pl.ds(pl.multiple_of(core * half, half), half), :]
    mine[...] = dcs[...] + dcr[1]
    s3 = remote(mine, mine, dsend.at[2], drecv.at[2], p, mate)
    s3.start()
    s3.wait_recv()
    for cp in gathers + firsts + sends + [s1, s2, s3] + lcopies:
        cp.wait_send()


def solution(mesh):
    np_, nd = mesh.shape["proto"], mesh.shape["data"]

    def step(emb_one, emb_two, protos):
        rows, dim = emb_one.shape
        kb = protos.shape[0]
        n, dma = np_ * nd, pltpu.SemaphoreType.DMA
        nx = (ITERS - 1) * 2 * nd
        vm, anym = pl.BlockSpec(memory_space=pltpu.VMEM), pl.BlockSpec(memory_space=pl.ANY)
        sds = jax.ShapeDtypeStruct
        out = pl.pallas_call(
            functools.partial(kernel, np_, nd),
            out_shape=(sds((rows, kb), F32), sds((rows, kb), F32), sds((1, 1), F32),
                       sds((rows, dim), F32), sds((rows, dim), F32), sds((kb, dim), F32)),
            in_specs=[anym] * 3,
            out_specs=(vm, vm, pl.BlockSpec(memory_space=pltpu.SMEM), vm, vm, vm),
            scratch_shapes=[
                pltpu.VMEM((2, rows, dim), jnp.bfloat16),
                pltpu.VMEM((np_, kb, dim), jnp.bfloat16),
                pltpu.VMEM((2, np_, rows, kb), F32),
                pltpu.VMEM((n, 2, kb), F32),
                pltpu.VMEM((nx, 1, np_ * kb), F32),
                pltpu.VMEM((2, rows, 128), F32),
                pltpu.VMEM((2, 128, np_ * kb), jnp.bfloat16),
                pltpu.VMEM((2, rows, kb), jnp.bfloat16),
                pltpu.VMEM((2, np_, 8, kb), F32),
                pltpu.VMEM((2, kb // 2, dim), F32),
                pltpu.VMEM((2, kb // 2, dim), F32),
                pltpu.VMEM((kb // 2, dim), F32),
                pltpu.VMEM((n, 1, 128), F32),
                dma((3,)), dma((np_,)), dma((np_,)), dma((n - 1,)), dma((n - 1,)),
                dma((nx,)), dma((nx,)), dma((3,)), dma((3,)), dma((n - 1,)), dma((n - 1,)),
            ],
            compiler_params=pltpu.CompilerParams(collective_id=0, has_side_effects=True,
                                                 vmem_limit_bytes=48 * 1024 * 1024),
        )(emb_one, emb_two, protos)
        code1, code2, loss, g1, g2, gc = out
        return code1, code2, loss.reshape(()), g1, g2, gc

    return jax.shard_map(
        step, mesh=mesh,
        in_specs=(P("data", None), P("data", None), P("proto", None)),
        out_specs=(P("data", "proto"), P("data", "proto"), P(), P("data", None), P("data", None), P("proto", None)),
        check_vma=False)
```

time: 275 us -> 75.3 us (0.27)
  blocking collectives: 129 us -> 0 us
  waiting for transfers between devices: 81.5 us -> 0 us
  Pallas kernels: 0 us -> 60.8 us
  other arithmetic: 25.6 us -> 0 us
  between operations: 17.3 us -> 2.5 us
  matrix products: 10.5 us -> 0 us
    psum x12 -> x0, blocking collectives: 129 us -> none  [the longest x6 65.3 us: view_terms(): row_sum = lax.psum(jnp.sum(transport, axis=1, keepdims=True), 'proto')]
    psum x2 -> x0, waiting for transfers between devices: 81.4 us -> none  [the longest x1 81.4 us: local_step(): lax.psum(jnp.einsum('nk,kd->nd', logit_grad_one, protos, preferred_elemen...]
    pallas_call x0 -> x1, Pallas kernels: none -> 60.8 us  [step(): pl.pallas_call(functools.partial(kernel, np_, nd), out_shape=(sds((rows,...]
    reduce_sum x11 -> x0, other arithmetic: 16.7 us -> none  [the longest x4 6 us: view_terms(): row_sum = lax.psum(jnp.sum(transport, axis=1, keepdims=True), 'proto')]
    dot_general x6 -> x0, matrix products: 10.5 us -> none  [the longest x2 3.93 us: view_terms(): jnp.einsum('nd,kd->nk', emb, protos, preferred_element_type=jnp.float32)]
    convert_element_type x2 -> x0, other arithmetic: 8.85 us -> none  [the longest x1 4.56 us: local_step(): ((jnp.exp(logp_one) - codes_two) / grad_scale).astype(jnp.bfloat16)]
    unnamed x27 -> x17, local copies, waits for them, and re-layouts: 11.3 us -> 11.7 us
  transfers between devices with their start and end apart: 2 -> 0, of which waited for: 1 -> 0; matrix products, arithmetic and copies ran while one was open for 5% -> 0% of each run, Pallas kernels for 0% -> 0%
where the time goes in v1:
time: 75.3 us; the launch traced here: 75 us
  Pallas kernels  60.8 us (81%)
  local copies, waits for them, and re-layouts  11.7 us (16%)
  between operations  2.5 us (3%)
    pallas_call x1, Pallas kernels, step(): pl.pallas_call(functools.partial(kernel, np_, nd), out_shape=(sds((rows,...  60.8 us
    unnamed x17, local copies, waits for them, and re-layouts  11.7 us

profile of v1, /device:TPU:0, one launch (start us, length us, event | category | flops | bytes accessed | tf_op | source)
XLA Modules:
  0.0 75.0 jit_solution(9132519817623351446)
XLA Ops:
  0.6 0.0 copy-start
  0.6 1.2 %copy-done = bf16[2048,256]{1,0:T(8,128)(2,1)S(1)} copy-done((bf16[2048,256]{1,0:T(8,128)(2,1)S(1)}, bf16[2048,256]{1,0:T(8,128)(2,1)}, u32[]{:S(2)}) %copy-start) | copy-done | bytes 1048600
  1.9 0.0 copy-start.1
  1.9 1.2 %copy-done.1 = bf16[2048,256]{1,0:T(8,128)(2,1)S(1)} copy-done((bf16[2048,256]{1,0:T(8,128)(2,1)S(1)}, bf16[2048,256]{1,0:T(8,128)(2,1)}, u32[]{:S(2)}) %copy-start.1) | copy-done | bytes 1048600
  3.1 0.0 copy-start.2
  3.1 0.9 %copy-done.2 = bf16[256,256]{1,0:T(8,128)(2,1)S(1)} copy-done((bf16[256,256]{1,0:T(8,128)(2,1)S(1)}, bf16[256,256]{1,0:T(8,128)(2,1)}, u32[]{:S(2)}) %copy-start.2) | copy-done | bytes 131096
  4.0 60.8 %shard_map.82 = (f32[2048,256]{1,0:T(8,128)S(1)}, f32[2048,256]{1,0:T(8,128)}, f32[1,1]{1,0:T(1,128)}, f32[2048,256]{1,0:T(8,128)}, f32[2048,256]{1,0:T(8,128)}, /*index=5*/f32[256,256]{1,0:T(8,128)S(1)}) custom-call(bf16[2048,256]{1,0:T(8,128)(2,1)S(1)} %copy-done, bf16[2048,256]{1,0:T(8,128)(2,1)S(1)} %copy-done.1, bf16[256,256]{1,0:T(8,128)(2,1)S(1)} %copy-done.2), custom_call_target="tpu_custom_call" | custom-call | tf_op jit(solution)/shard_map/pallas_call | solution.py:251
  64.8 0.0 copy-start.5
  64.8 1.3 %copy.15 = f32[2048,256]{1,0:T(8,128)} copy(f32[2048,256]{1,0:T(8,128)S(1)} %get-tuple-element.24) | data formatting | bytes 4194304
  66.1 1.0 %copy-done.5 = f32[2048,256]{1,0:T(8,128)S(1)} copy-done((f32[2048,256]{1,0:T(8,128)S(1)}, f32[2048,256]{1,0:T(8,128)}, u32[]{:S(2)}) %copy-start.5) | copy-done | bytes 2097176
  67.1 0.0 copy-start.4
  67.1 1.3 %copy.16 = f32[2048,256]{1,0:T(8,128)} copy(f32[2048,256]{1,0:T(8,128)S(1)} %copy-done.5) | data formatting | bytes 4194304
  69.2 0.3 copy-done.4
  69.5 0.0 copy-start.3
  69.5 1.3 %copy.18 = f32[2048,256]{1,0:T(8,128)} copy(f32[2048,256]{1,0:T(8,128)S(1)} %copy-done.4) | data formatting | bytes 4194304
  70.8 1.0 %copy-done.3 = f32[2048,256]{1,0:T(8,128)S(1)} copy-done((f32[2048,256]{1,0:T(8,128)S(1)}, f32[2048,256]{1,0:T(8,128)}, u32[]{:S(2)}) %copy-start.3) | copy-done | bytes 2097176
  71.8 1.3 %copy.19 = f32[2048,256]{1,0:T(8,128)} copy(f32[2048,256]{1,0:T(8,128)S(1)} %copy-done.3) | data formatting | bytes 4194304
  73.2 0.7 copy.20
Async XLA Ops:
  0.6 1.2 %copy-start = (bf16[2048,256]{1,0:T(8,128)(2,1)S(1)}, bf16[2048,256]{1,0:T(8,128)(2,1)}, u32[]{:S(2)}) copy-start(bf16[2048,256]{1,0:T(8,128)(2,1)} %z1_ref.1) | copy-start | bytes 3145732
  1.9 1.2 %copy-start.1 = (bf16[2048,256]{1,0:T(8,128)(2,1)S(1)}, bf16[2048,256]{1,0:T(8,128)(2,1)}, u32[]{:S(2)}) copy-start(bf16[2048,256]{1,0:T(8,128)(2,1)} %z2_ref.1) | copy-start | bytes 3145732
  3.1 0.9 %copy-start.2 = (bf16[256,256]{1,0:T(8,128)(2,1)S(1)}, bf16[256,256]{1,0:T(8,128)(2,1)}, u32[]{:S(2)}) copy-start(bf16[256,256]{1,0:T(8,128)(2,1)} %c_ref.1) | copy-start | bytes 393220
  64.8 2.3 %copy-start.5 = (f32[2048,256]{1,0:T(8,128)S(1)}, f32[2048,256]{1,0:T(8,128)}, u32[]{:S(2)}) copy-start(f32[2048,256]{1,0:T(8,128)} %get-tuple-element.25) | copy-start | bytes 6291460
  67.1 2.3 %copy-start.4 = (f32[2048,256]{1,0:T(8,128)S(1)}, f32[2048,256]{1,0:T(8,128)}, u32[]{:S(2)}) copy-start(f32[2048,256]{1,0:T(8,128)} %get-tuple-element.27) | copy-start | bytes 6291460
  69.5 2.3 %copy-start.3 = (f32[2048,256]{1,0:T(8,128)S(1)}, f32[2048,256]{1,0:T(8,128)}, u32[]{:S(2)}) copy-start(f32[2048,256]{1,0:T(8,128)} %get-tuple-element.28) | copy-start | bytes 6291460

commit v2 on v1

v2 whole, which is shorter than its diff:
```python
import functools
import math

import jax
import jax.numpy as jnp
from jax import lax
from jax.experimental import pallas as pl
from jax.experimental.pallas import tpu as pltpu
from jax.sharding import PartitionSpec as P

EPSILON = 0.05
TEMP_TAU = 0.1
ITERS = 3
VMEM_MIB = 48
MESH = pl.DeviceIdType.MESH
F32 = jnp.float32
LOG2E = math.log2(math.e)


def lanes(x):
    total = x[:, :128]
    for i in range(1, x.shape[1] // 128):
        total = total + x[:, i * 128:(i + 1) * 128]
    return total


def subl(x):
    return jnp.sum(x.reshape(x.shape[0] // 8, 8, x.shape[1]), axis=0)


def kernel(np_, nd, z1_ref, z2_ref, c_ref,
           code1, code2, loss_ref, g1, g2, gc,
           z, call, e, a2, c1b, cb, dsum, di, rs, hown, vb, dcp, dcr, dcs, lossb,
           lsem, csend, crecv, fsend, frecv, c1send, c1recv, bsend, brecv, dsend, drecv, lsend, lrecv):
    rows, kb = z.shape[1], 2 * call.shape[2]
    nrows, nk = rows * nd, kb * np_
    p, d = lax.axis_index("proto"), lax.axis_index("data")
    core = d % 2
    mate, across = d + 1 - 2 * core, (d + 2) % nd
    codes, grads = (code1, code2), (g1, g2)
    near = p + 1 - 2 * (p % 2)
    peers = (near, (p + 2) % np_, (near + 2) % np_)

    def remote(src, dst, ss, rsem, pp, dd):
        return pltpu.make_async_remote_copy(src_ref=src, dst_ref=dst, send_sem=ss, recv_sem=rsem,
                                            device_id={"proto": pp, "data": dd}, device_id_type=MESH)

    half = kb // 2
    loads = [pltpu.make_async_copy(c_ref.at[pl.ds(0, half), :], call.at[p, 0], lsem.at[0]),
             pltpu.make_async_copy(c_ref.at[pl.ds(half, half), :], call.at[p, 1], lsem.at[1]),
             pltpu.make_async_copy(z1_ref, z.at[0], lsem.at[2]),
             pltpu.make_async_copy(z2_ref, z.at[1], lsem.at[3])]
    for cp in loads:
        cp.start()
    others = [(i, j) for i in range(np_) for j in range(nd) if i or j]
    barrier = pltpu.get_barrier_semaphore()
    for i, j in others:
        pl.semaphore_signal(barrier, inc=1, device_id={"proto": (p + i) % np_, "data": (d + j) % nd},
                            device_id_type=MESH)
    loads[0].wait()
    loads[1].wait()
    pl.semaphore_wait(barrier, len(others))

    gathers = []
    for n, peer in enumerate(peers):
        cp = remote(call.at[p, core], call.at[p, core], csend.at[n], crecv.at[n], peer, d)
        cp.start()
        gathers.append(cp)

    def scores(v, b, r):
        return lax.dot_general(z[v, r, :], call[b].reshape(kb, call.shape[3]), (((1,), (1,)), ((), ())),
                               preferred_element_type=F32)

    def chunk(i, size):
        return pl.ds(pl.multiple_of(i * size, size), size)

    RC = 512

    def exp_block(v, b, n):
        def body(i, acc):
            r = chunk(i, RC)
            x = jnp.exp2(scores(v, b, r) * (LOG2E / TEMP_TAU))
            e[v, b, r, :] = x
            s = lanes(x)
            dsum[v, n // 2, r, :] = dsum[v, n // 2, r, :] + s if n % 2 else s
            x = x * x
            a2[v, b, r, :] = x
            return acc + subl(x) if n == 0 else acc
        return lax.fori_loop(0, rows // RC, body, jnp.zeros((8, kb), F32))

    own = []
    for v in range(2):
        loads[2 + v].wait()
        own.append(jnp.sum(exp_block(v, p, 0), axis=0, keepdims=True))
    c1b[d * np_ + p] = jnp.concatenate(own, axis=0)
    firsts = []
    for n, (i, j) in enumerate(others):
        me = c1b.at[d * np_ + p]
        cp = remote(me, me, c1send.at[n], c1recv.at[n], (p + i) % np_, (d + j) % nd)
        cp.start()
        firsts.append(cp)

    forwards = []
    for n, b in enumerate(peers):
        got = remote(call.at[b, core], call.at[b, core], csend.at[n], crecv.at[n], b, d)
        got.wait_recv()
        cp = remote(call.at[b, core], call.at[b, core], fsend.at[n], frecv.at[n], p, mate)
        cp.start()
        forwards.append(cp)
    for n, b in enumerate(peers):
        got = remote(call.at[b, 1 - core], call.at[b, 1 - core], fsend.at[n], frecv.at[n], p, mate)
        got.wait_recv()
        for v in range(2):
            exp_block(v, b, n + 1)
    for cp in firsts:
        cp.wait_recv()
    for v in range(2):
        for b in range(np_):
            tot = c1b[b, v:v + 1, :]
            for j in range(1, nd):
                tot = tot + c1b[j * np_ + b, v:v + 1, :]
            vb[v, b] = jnp.broadcast_to(1.0 / (nk * tot), (8, kb))

    def scaled(v, b, r):
        n = r.size // 8
        return (a2[v, b, r, :].reshape(n, 8, kb) * vb[v, b][None]).reshape(n * 8, kb)

    def rowsum(v, r):
        acc = lanes(scaled(v, 0, r))
        for b in range(1, np_):
            acc = acc + lanes(scaled(v, b, r))
        return jnp.sum(acc, axis=1, keepdims=True)

    R2 = 128

    def sweep(v):
        def body(i, accs):
            r = chunk(i, R2)
            u = 1.0 / (nrows * rowsum(v, r))
            return tuple(accs[b] + subl(a2[v, b, r, :] * u) for b in range(np_))
        return lax.fori_loop(0, rows // R2, body, tuple(jnp.zeros((8, kb), F32) for _ in range(np_)))

    def exchange(it, v, accs):
        slot = (it * 2 + v) * nd
        for b in range(np_):
            cb[slot + d, :, b * kb:(b + 1) * kb] = jnp.sum(accs[b], axis=0, keepdims=True)
        out = []
        for q in range(1, nd):
            me = cb.at[slot + d]
            cp = remote(me, me, bsend.at[slot + q], brecv.at[slot + q], p, (d + q) % nd)
            cp.start()
            out.append(cp)
        return out

    def finish(it, v, copies):
        slot = (it * 2 + v) * nd
        for cp in copies:
            cp.wait_recv()
        tot = cb[slot]
        for j in range(1, nd):
            tot = tot + cb[slot + j]
        inv = 1.0 / (nk * tot)
        for b in range(np_):
            vb[v, b] = jnp.broadcast_to(inv[:, b * kb:(b + 1) * kb], (8, kb))

    scale = 1.0 / (2 * nrows * TEMP_TAU)

    def wide(x):
        return jnp.concatenate([x, x], axis=1)

    R3 = 128

    def own_part(v, lacc):
        w = 1 - v

        def body(i, lacc):
            r = chunk(i, R3)
            rinv = jnp.broadcast_to(1.0 / rowsum(v, r), (R3, 128))
            rsc = rinv * scale
            rs[v, r, :] = rsc
            den = jnp.broadcast_to(jnp.sum(dsum[w, 0, r, :] + dsum[w, 1, r, :], axis=1, keepdims=True), (R3, 128))
            dsc = scale / den
            di[w, r, :] = dsc
            t = scaled(v, p, r)
            q = t * wide(rinv)
            codes[v][r, :] = q
            hown[w, r, :] = (e[w, p, r, :] * wide(dsc) - t * wide(rsc)).astype(jnp.bfloat16)
            logp = scores(w, p, r) * (1.0 / TEMP_TAU) - wide(jnp.log(den))
            return lacc + subl(lanes(q * logp))

        return lax.fori_loop(0, rows // R3, body, lacc)

    def dc_part(w):
        return lax.dot_general(hown[w], z[w], (((0,), (0,)), ((), ())), preferred_element_type=F32)

    pend, sends = [None, None], []
    for it in range(ITERS - 1):
        for v in range(2):
            if it:
                finish(it - 1, v, pend[v])
            pend[v] = exchange(it, v, sweep(v))
            sends += pend[v]
    lacc = jnp.zeros((8, 128), F32)
    finish(ITERS - 2, 0, pend[0])
    lacc = own_part(0, lacc)
    finish(ITERS - 2, 1, pend[1])
    lacc = own_part(1, lacc)
    dcp[...] = (dc_part(0) + dc_part(1)).reshape(dcp.shape)

    s1 = remote(dcp.at[1 - core], dcr.at[0], dsend.at[0], drecv.at[0], p, mate)
    s1.start()
    lossb[d * np_ + p] = jnp.broadcast_to(jnp.sum(lacc).reshape(1, 1), (1, 128))
    lcopies = []
    for n, (i, j) in enumerate(others):
        me = lossb.at[d * np_ + p]
        cp = remote(me, me, lsend.at[n], lrecv.at[n], (p + i) % np_, (d + j) % nd)
        cp.start()
        lcopies.append(cp)

    def grad_part(lo, hi):
        def body(i, carry):
            r = chunk(i, R3)
            acc = None
            for b in range(np_):
                hs = [e[w, b, r, :] * wide(di[w, r, :]) - scaled(1 - w, b, r) * wide(rs[1 - w, r, :]) for w in range(2)]
                x = jnp.dot(jnp.concatenate(hs, axis=0).astype(jnp.bfloat16), call[b].reshape(kb, call.shape[3]),
                            preferred_element_type=F32)
                acc = x if acc is None else acc + x
            for w in range(2):
                grads[w][r, :] = acc[w * R3:(w + 1) * R3]
            return carry
        lax.fori_loop(lo, hi, body, 0)

    steps = rows // R3
    cut = steps // 4
    grad_part(0, cut)
    s1.wait_recv()
    dcs[...] = dcp[core] + dcr[0]
    s2 = remote(dcs, dcr.at[1], dsend.at[1], drecv.at[1], p, across)
    s2.start()
    grad_part(cut, steps)
    for cp in lcopies:
        cp.wait_recv()
    tot = lossb[0]
    for n in range(1, np_ * nd):
        tot = tot + lossb[n]
    loss_ref[0, 0] = jnp.sum(tot[:, :1]) * (-1.0 / (2 * nrows))
    s2.wait_recv()
    mine = gc.at[pl.ds(pl.multiple_of(core * half, half), half), :]
    mine[...] = dcs[...] + dcr[1]
    s3 = remote(mine, mine, dsend.at[2], drecv.at[2], p, mate)
    s3.start()
    s3.wait_recv()
    for cp in gathers + firsts + forwards + sends + [s1, s2, s3] + lcopies:
        cp.wait_send()


def write_out(*refs):
    n = (len(refs) - 1) // 2
    copies = [pltpu.make_async_copy(refs[i], refs[n + i], refs[-1].at[i]) for i in range(n)]
    for cp in copies:
        cp.start()
    for cp in copies:
        cp.wait()


def solution(mesh):
    np_, nd = mesh.shape["proto"], mesh.shape["data"]

    def step(emb_one, emb_two, protos):
        rows, dim = emb_one.shape
        kb = protos.shape[0]
        n, dma = np_ * nd, pltpu.SemaphoreType.DMA
        nx = (ITERS - 1) * 2 * nd
        vm, hbm = pl.BlockSpec(memory_space=pltpu.VMEM), pl.BlockSpec(memory_space=pltpu.HBM)
        sds = jax.ShapeDtypeStruct
        code1, code2, loss, g1, g2, gc = pl.pallas_call(
            functools.partial(kernel, np_, nd),
            out_shape=(pltpu.VMEM((rows, kb), F32), pltpu.VMEM((rows, kb), F32), sds((1, 1), F32),
                       pltpu.VMEM((rows, dim), F32), pltpu.VMEM((rows, dim), F32), pltpu.VMEM((kb, dim), F32)),
            in_specs=[hbm] * 3,
            out_specs=(vm, vm, pl.BlockSpec(memory_space=pltpu.SMEM), vm, vm, vm),
            scratch_shapes=[
                pltpu.VMEM((2, rows, dim), jnp.bfloat16),
                pltpu.VMEM((np_, 2, kb // 2, dim), jnp.bfloat16),
                pltpu.VMEM((2, np_, rows, kb), F32),
                pltpu.VMEM((2, np_, rows, kb), F32),
                pltpu.VMEM((n, 2, kb), F32),
                pltpu.VMEM((nx, 1, np_ * kb), F32),
                pltpu.VMEM((2, 2, rows, 128), F32),
                pltpu.VMEM((2, rows, 128), F32),
                pltpu.VMEM((2, rows, 128), F32),
                pltpu.VMEM((2, rows, kb), jnp.bfloat16),
                pltpu.VMEM((2, np_, 8, kb), F32),
                pltpu.VMEM((2, kb // 2, dim), F32),
                pltpu.VMEM((2, kb // 2, dim), F32),
                pltpu.VMEM((kb // 2, dim), F32),
                pltpu.VMEM((n, 1, 128), F32),
                dma((4,)), dma((3,)), dma((3,)), dma((3,)), dma((3,)), dma((n - 1,)), dma((n - 1,)),
                dma((nx,)), dma((nx,)), dma((3,)), dma((3,)), dma((n - 1,)), dma((n - 1,)),
            ],
            compiler_params=pltpu.CompilerParams(collective_id=0, has_side_effects=True,
                                                 vmem_limit_bytes=VMEM_MIB * 1024 * 1024),
        )(*(pltpu.with_memory_space_constraint(x, pltpu.HBM) for x in (emb_one, emb_two, protos)))
        big = (code1, code2, g1, g2, gc)
        code1, code2, g1, g2, gc = pl.pallas_call(
            write_out,
            out_shape=tuple(sds(x.shape, F32) for x in big),
            in_specs=[vm] * len(big),
            out_specs=(hbm,) * len(big),
            scratch_shapes=[dma((len(big),))],
            compiler_params=pltpu.CompilerParams(vmem_limit_bytes=1024 * 1024),
        )(*big)
        return code1, code2, loss.reshape(()), g1, g2, gc

    return jax.shard_map(
        step, mesh=mesh,
        in_specs=(P("data", None), P("data", None), P("proto", None)),
        out_specs=(P("data", "proto"), P("data", "proto"), P(), P("data", None), P("data", None), P("proto", None)),
        check_vma=False)
```

time: 75.3 us -> 48.1 us (0.64)
  Pallas kernels: 60.8 us -> 45.6 us
  local copies, waits for them, and re-layouts: 11.7 us -> 0 us
    pallas_call x1 -> x2, Pallas kernels: 60.8 us -> 45.6 us  [the longest x1 42.2 us: step(): pl.pallas_call(functools.partial(kernel, np_, nd), out_shape=(pltpu.VMEM(...]
    unnamed x17 -> x0, local copies, waits for them, and re-layouts: 11.7 us -> none
where the time goes in v2:
time: 48.1 us; the launch traced here: 48 us
  Pallas kernels  45.6 us (95%)
  between operations  2.41 us (5%)
    pallas_call x1, Pallas kernels, step(): pl.pallas_call(functools.partial(kernel, np_, nd), out_shape=(pltpu.VMEM(...  42.2 us
    pallas_call x1, Pallas kernels, step(): pl.pallas_call(write_out, out_shape=tuple((sds(x.shape, F32) for x in big...  3.39 us

profile of v2, /device:TPU:0, one launch (start us, length us, event | category | flops | bytes accessed | tf_op | source)
XLA Modules:
  0.0 48.0 jit_solution(4128557893260782634)
XLA Ops:
  0.6 42.2 %shard_map.82 = (f32[2048,256]{1,0:T(8,128)S(1)}, f32[2048,256]{1,0:T(8,128)S(1)}, f32[1,1]{1,0:T(1,128)}, f32[2048,256]{1,0:T(8,128)S(1)}, f32[2048,256]{1,0:T(8,128)S(1)}, /*index=5*/f32[256,256]{1,0:T(8,128)S(1)}) custom-call(bf16[2048,256]{1,0:T(8,128)(2,1)} %z1_ref.1, bf16[2048,256]{1,0:T(8,128)(2,1)} %z2_ref.1, bf16[256,256]{1,0:T(8,128)(2,1)} %c_ref.1), custom_call_target="tpu_custom_call" | custom-call | tf_op jit(solution)/shard_map/pallas_call | solution.py:277
  42.8 3.4 %shard_map.83 = (f32[2048,256]{1,0:T(8,128)}, f32[2048,256]{1,0:T(8,128)}, f32[2048,256]{1,0:T(8,128)}, f32[2048,256]{1,0:T(8,128)}, f32[256,256]{1,0:T(8,128)}) custom-call(f32[2048,256]{1,0:T(8,128)S(1)} %get-tuple-element.17.refs_0_, f32[2048,256]{1,0:T(8,128)S(1)} %get-tuple-element.18.refs_1_, f32[2048,256]{1,0:T(8,128)S(1)} %get-tuple-element.19.refs_2_, ...), custom_call_target="tpu_custom_call" | custom-call | tf_op jit(solution)/shard_map/pallas_call | solution.py:306

commit v3 on v2

v3 whole, which is shorter than its diff:
```python
import functools
import math

import jax
import jax.numpy as jnp
from jax import lax
from jax.experimental import pallas as pl
from jax.experimental.pallas import tpu as pltpu
from jax.sharding import PartitionSpec as P

EPSILON = 0.05
TEMP_TAU = 0.1
ITERS = 3
VMEM_MIB = 40
MESH = pl.DeviceIdType.MESH
F32 = jnp.float32
LOG2E = math.log2(math.e)


def lanes(x):
    total = x[:, :128]
    for i in range(1, x.shape[1] // 128):
        total = total + x[:, i * 128:(i + 1) * 128]
    return total


def subl(x):
    return jnp.sum(x.reshape(x.shape[0] // 8, 8, x.shape[1]), axis=0)


def kernel(np_, nd, z1_ref, z2_ref, c_ref,
           code1, code2, loss_ref, g1, g2, gc,
           z, call, a2, c1b, c1t, cb, dsum, di, rs, hown, vb, dcp, dcr, dcs, lossb, losst,
           lsem, csend, crecv, fsend, frecv, bsend, brecv, dsend, drecv, tsend, trecv):
    rows, kb = z.shape[1], 2 * call.shape[2]
    nrows, nk = rows * nd, kb * np_
    p, d = lax.axis_index("proto"), lax.axis_index("data")
    core = d % 2
    mate, across = d + 1 - 2 * core, (d + 2) % nd
    codes, grads = (code1, code2), (g1, g2)
    near = p + 1 - 2 * (p % 2)
    peers = (near, (p + 2) % np_, (near + 2) % np_)

    def remote(src, dst, ss, rsem, pp, dd):
        return pltpu.make_async_remote_copy(src_ref=src, dst_ref=dst, send_sem=ss, recv_sem=rsem,
                                            device_id={"proto": pp, "data": dd}, device_id_type=MESH)

    half = kb // 2
    loads = [pltpu.make_async_copy(c_ref.at[pl.ds(0, half), :], call.at[p, 0], lsem.at[0]),
             pltpu.make_async_copy(c_ref.at[pl.ds(half, half), :], call.at[p, 1], lsem.at[1]),
             pltpu.make_async_copy(z1_ref, z.at[0], lsem.at[2]),
             pltpu.make_async_copy(z2_ref, z.at[1], lsem.at[3])]
    for cp in loads:
        cp.start()
    ring = [(d + j) % nd for j in range(1, nd)]
    barrier = pltpu.get_barrier_semaphore()
    for pp, dd in [(b, d) for b in peers] + [(p, j) for j in ring]:
        pl.semaphore_signal(barrier, inc=1, device_id={"proto": pp, "data": dd}, device_id_type=MESH)
    loads[0].wait()
    loads[1].wait()
    pl.semaphore_wait(barrier, np_ + nd - 2)

    gathers = []
    for n, peer in enumerate(peers):
        cp = remote(call.at[p, core], call.at[p, core], csend.at[n], crecv.at[n], peer, d)
        cp.start()
        gathers.append(cp)

    def scores(v, b, r):
        return lax.dot_general(z[v, r, :], call[b].reshape(kb, call.shape[3]), (((1,), (1,)), ((), ())),
                               preferred_element_type=F32)

    def chunk(i, size):
        return pl.ds(pl.multiple_of(i * size, size), size)

    def to_data(me, slot):
        out = []
        for q, dd in enumerate(ring):
            cp = remote(me, me, bsend.at[slot + q], brecv.at[slot + q], p, dd)
            cp.start()
            out.append(cp)
        return out

    def to_proto(me, k):
        out = []
        for n, b in enumerate(peers):
            cp = remote(me, me, tsend.at[k + n], trecv.at[k + n], b, d)
            cp.start()
            out.append(cp)
        return out

    def arrived(copies):
        for cp in copies:
            cp.wait_recv()

    RC = 256

    def exp_block(v, b, n):
        def body(i, acc):
            for r in (chunk(2 * i, RC), chunk(2 * i + 1, RC)):
                x = jnp.exp2(scores(v, b, r) * (LOG2E / TEMP_TAU))
                t = lanes(x)
                dsum[v, n // 2, r, :] = dsum[v, n // 2, r, :] + t if n % 2 else t
                x = x * x
                a2[v, b, r, :] = x
                if n == 0:
                    acc = acc + subl(x)
            return acc
        return lax.fori_loop(0, rows // RC // 2, body, jnp.zeros((8, kb), F32))

    own = []
    for v in range(2):
        loads[2 + v].wait()
        own.append(jnp.sum(exp_block(v, p, 0), axis=0, keepdims=True))
    c1b[d] = jnp.concatenate(own, axis=0)
    firsts = to_data(c1b.at[d], 0)

    forwards = []

    def forward(n):
        b = peers[n]
        remote(call.at[b, core], call.at[b, core], csend.at[n], crecv.at[n], b, d).wait_recv()
        cp = remote(call.at[b, core], call.at[b, core], fsend.at[n], frecv.at[n], p, mate)
        cp.start()
        forwards.append(cp)

    def use(n):
        b = peers[n]
        remote(call.at[b, 1 - core], call.at[b, 1 - core], fsend.at[n], frecv.at[n], p, mate).wait_recv()
        for v in range(2):
            exp_block(v, b, n + 1)

    def total(ref, n):
        tot = ref[0]
        for j in range(1, n):
            tot = tot + ref[j]
        return tot

    forward(0)
    forward(1)
    arrived(firsts)
    c1t[p] = total(c1b, nd)
    seconds = to_proto(c1t.at[p], 0)
    use(0)
    forward(2)
    use(1)
    use(2)
    arrived(seconds)
    for v in range(2):
        for b in range(np_):
            vb[v, b] = jnp.broadcast_to(1.0 / (nk * c1t[b, v:v + 1, :]), (8, kb))

    def scaled(v, b, r):
        n = r.size // 8
        return (a2[v, b, r, :].reshape(n, 8, kb) * vb[v, b][None]).reshape(n * 8, kb)

    def rowsum(v, r):
        acc = lanes(scaled(v, 0, r))
        for b in range(1, np_):
            acc = acc + lanes(scaled(v, b, r))
        return jnp.sum(acc, axis=1, keepdims=True)

    R2 = 128

    def sweep(v):
        def body(i, accs):
            r = chunk(i, R2)
            u = 1.0 / (nrows * rowsum(v, r))
            return tuple(accs[b] + subl(a2[v, b, r, :] * u) for b in range(np_))
        return lax.fori_loop(0, rows // R2, body, tuple(jnp.zeros((8, kb), F32) for _ in range(np_)))

    def exchange(it, v, accs):
        slot = it * 2 + v
        for b in range(np_):
            cb[slot * nd + d, :, b * kb:(b + 1) * kb] = jnp.sum(accs[b], axis=0, keepdims=True)
        return to_data(cb.at[slot * nd + d], (slot + 1) * (nd - 1))

    def finish(it, v, copies):
        arrived(copies)
        tot = cb[(it * 2 + v) * nd]
        for j in range(1, nd):
            tot = tot + cb[(it * 2 + v) * nd + j]
        inv = 1.0 / (nk * tot)
        for b in range(np_):
            vb[v, b] = jnp.broadcast_to(inv[:, b * kb:(b + 1) * kb], (8, kb))

    scale = 1.0 / (2 * nrows * TEMP_TAU)

    def wide(x):
        return jnp.concatenate([x, x], axis=1)

    R3 = 128

    def dens():
        def body(i, carry):
            r = chunk(i, R3)
            for v in range(2):
                den = jnp.sum(dsum[v, 0, r, :] + dsum[v, 1, r, :], axis=1, keepdims=True)
                di[v, r, :] = jnp.broadcast_to(scale / den, (R3, 128))
                dsum[v, 0, r, :] = jnp.broadcast_to(jnp.log(den), (R3, 128))
            return carry
        lax.fori_loop(0, rows // R3, body, 0)

    R4 = 256

    def own_part(v, lacc):
        w = 1 - v

        def body(i, lacc):
            r = chunk(i, R4)
            rinv = jnp.broadcast_to(1.0 / rowsum(v, r), (R4, 128))
            rsc = rinv * scale
            rs[v, r, :] = rsc
            t = scaled(v, p, r)
            q = t * wide(rinv)
            codes[v][r, :] = q
            x = a2[w, p, r, :]
            hw = (x * lax.rsqrt(x) * wide(di[w, r, :]) - t * wide(rsc)).astype(jnp.bfloat16)
            hown[w, 0, r, :] = hw[:, :half]
            hown[w, 1, r, :] = hw[:, half:]
            logp = scores(w, p, r) * (1.0 / TEMP_TAU) - wide(dsum[w, 0, r, :])
            return lacc + subl(lanes(q * logp))

        return lax.fori_loop(0, rows // R4, body, lacc)

    def dc_part(w, k):
        return lax.dot_general(hown[w, k], z[w], (((0,), (0,)), ((), ())), preferred_element_type=F32)

    pend, sends = [None, None], []
    for it in range(ITERS - 1):
        for v in range(2):
            if it:
                finish(it - 1, v, pend[v])
            pend[v] = exchange(it, v, sweep(v))
            sends += pend[v]
        if it == 0:
            dens()
    lacc = jnp.zeros((8, 128), F32)
    finish(ITERS - 2, 0, pend[0])
    lacc = own_part(0, lacc)
    finish(ITERS - 2, 1, pend[1])
    lacc = own_part(1, lacc)
    dcp[0] = dc_part(0, 1 - core) + dc_part(1, 1 - core)
    s1 = remote(dcp.at[0], dcr.at[0], dsend.at[0], drecv.at[0], p, mate)
    s1.start()
    lossb[d] = jnp.broadcast_to(jnp.sum(lacc).reshape(1, 1), (1, 128))
    lcopies = to_data(lossb.at[d], (2 * ITERS - 1) * (nd - 1))
    dcp[1] = dc_part(0, core) + dc_part(1, core)

    def root(v, b, r):
        x = a2[v, b, r, :]
        return x * lax.rsqrt(x)

    def grad_part(lo, hi):
        def body(i, carry):
            r = chunk(i, R3)
            acc = None
            for b in range(np_):
                hs = [root(w, b, r) * wide(di[w, r, :]) - scaled(1 - w, b, r) * wide(rs[1 - w, r, :]) for w in range(2)]
                x = jnp.dot(jnp.concatenate(hs, axis=0).astype(jnp.bfloat16), call[b].reshape(kb, call.shape[3]),
                            preferred_element_type=F32)
                acc = x if acc is None else acc + x
            for w in range(2):
                grads[w][r, :] = acc[w * R3:(w + 1) * R3]
            return carry
        lax.fori_loop(lo, hi, body, 0)

    steps = rows // R3
    cut = steps // 4
    grad_part(0, cut)
    s1.wait_recv()
    dcs[...] = dcp[1] + dcr[0]
    s2 = remote(dcs, dcr.at[1], dsend.at[1], drecv.at[1], p, across)
    s2.start()
    arrived(lcopies)
    losst[p] = total(lossb, nd)
    lfinal = to_proto(losst.at[p], np_ - 1)
    grad_part(cut, steps)
    arrived(lfinal)
    loss_ref[0, 0] = jnp.sum(total(losst, np_)[:, :1]) * (-1.0 / (2 * nrows))
    s2.wait_recv()
    mine = gc.at[pl.ds(pl.multiple_of(core * half, half), half), :]
    mine[...] = dcs[...] + dcr[1]
    s3 = remote(mine, mine, dsend.at[2], drecv.at[2], p, mate)
    s3.start()
    s3.wait_recv()
    for cp in gathers + firsts + seconds + forwards + sends + [s1, s2, s3] + lcopies + lfinal:
        cp.wait_send()


def write_out(*refs):
    n = (len(refs) - 1) // 2
    copies = [pltpu.make_async_copy(refs[i], refs[n + i], refs[-1].at[i]) for i in range(n)]
    for cp in copies:
        cp.start()
    for cp in copies:
        cp.wait()


def solution(mesh):
    np_, nd = mesh.shape["proto"], mesh.shape["data"]

    def step(emb_one, emb_two, protos):
        rows, dim = emb_one.shape
        kb = protos.shape[0]
        dma = pltpu.SemaphoreType.DMA
        nx, nsem = (ITERS - 1) * 2 * nd, 2 * ITERS * (nd - 1)
        vm, hbm = pl.BlockSpec(memory_space=pltpu.VMEM), pl.BlockSpec(memory_space=pltpu.HBM)
        sds = jax.ShapeDtypeStruct
        code1, code2, loss, g1, g2, gc = pl.pallas_call(
            functools.partial(kernel, np_, nd),
            out_shape=(pltpu.VMEM((rows, kb), F32), pltpu.VMEM((rows, kb), F32), sds((1, 1), F32),
                       pltpu.VMEM((rows, dim), F32), pltpu.VMEM((rows, dim), F32), pltpu.VMEM((kb, dim), F32)),
            in_specs=[hbm] * 3,
            out_specs=(vm, vm, pl.BlockSpec(memory_space=pltpu.SMEM), vm, vm, vm),
            scratch_shapes=[
                pltpu.VMEM((2, rows, dim), jnp.bfloat16),
                pltpu.VMEM((np_, 2, kb // 2, dim), jnp.bfloat16),
                pltpu.VMEM((2, np_, rows, kb), F32),
                pltpu.VMEM((nd, 2, kb), F32),
                pltpu.VMEM((np_, 2, kb), F32),
                pltpu.VMEM((nx, 1, np_ * kb), F32),
                pltpu.VMEM((2, 2, rows, 128), F32),
                pltpu.VMEM((2, rows, 128), F32),
                pltpu.VMEM((2, rows, 128), F32),
                pltpu.VMEM((2, 2, rows, kb // 2), jnp.bfloat16),
                pltpu.VMEM((2, np_, 8, kb), F32),
                pltpu.VMEM((2, kb // 2, dim), F32),
                pltpu.VMEM((2, kb // 2, dim), F32),
                pltpu.VMEM((kb // 2, dim), F32),
                pltpu.VMEM((nd, 1, 128), F32),
                pltpu.VMEM((np_, 1, 128), F32),
                dma((4,)), dma((np_ - 1,)), dma((np_ - 1,)), dma((np_ - 1,)), dma((np_ - 1,)),
                dma((nsem,)), dma((nsem,)), dma((3,)), dma((3,)), dma((2 * np_ - 2,)), dma((2 * np_ - 2,)),
            ],
            compiler_params=pltpu.CompilerParams(collective_id=0, has_side_effects=True,
                                                 vmem_limit_bytes=VMEM_MIB * 1024 * 1024),
        )(*(pltpu.with_memory_space_constraint(x, pltpu.HBM) for x in (emb_one, emb_two, protos)))
        big = (code1, code2, g1, g2, gc)
        code1, code2, g1, g2, gc = pl.pallas_call(
            write_out,
            out_shape=tuple(sds(x.shape, F32) for x in big),
            in_specs=[vm] * len(big),
            out_specs=(hbm,) * len(big),
            scratch_shapes=[dma((len(big),))],
            compiler_params=pltpu.CompilerParams(vmem_limit_bytes=1024 * 1024),
        )(*big)
        return code1, code2, loss.reshape(()), g1, g2, gc

    return jax.shard_map(
        step, mesh=mesh,
        in_specs=(P("data", None), P("data", None), P("proto", None)),
        out_specs=(P("data", "proto"), P("data", "proto"), P(), P("data", None), P("data", None), P("proto", None)),
        check_vma=False)
```

time: 48.1 us -> 47.9 us (level)
  no operation moved by 1% of the time
where the time goes in v3:
time: 47.9 us; the launch traced here: 47.8 us
  Pallas kernels  45.4 us (95%)
  between operations  2.41 us (5%)
    pallas_call x1, Pallas kernels, step(): pl.pallas_call(functools.partial(kernel, np_, nd), out_shape=(pltpu.VMEM(...  42 us
    pallas_call x1, Pallas kernels, step(): pl.pallas_call(write_out, out_shape=tuple((sds(x.shape, F32) for x in big...  3.39 us

profile of v3, /device:TPU:0, one launch (start us, length us, event | category | flops | bytes accessed | tf_op | source)
XLA Modules:
  0.0 47.8 jit_solution(15890270712844876678)
XLA Ops:
  0.6 42.0 %shard_map.82 = (f32[2048,256]{1,0:T(8,128)S(1)}, f32[2048,256]{1,0:T(8,128)S(1)}, f32[1,1]{1,0:T(1,128)}, f32[2048,256]{1,0:T(8,128)S(1)}, f32[2048,256]{1,0:T(8,128)S(1)}, /*index=5*/f32[256,256]{1,0:T(8,128)S(1)}) custom-call(bf16[2048,256]{1,0:T(8,128)(2,1)} %z1_ref.1, bf16[2048,256]{1,0:T(8,128)(2,1)} %z2_ref.1, bf16[256,256]{1,0:T(8,128)(2,1)} %c_ref.1), custom_call_target="tpu_custom_call" | custom-call | tf_op jit(solution)/shard_map/pallas_call | solution.py:310
  42.6 3.4 %shard_map.83 = (f32[2048,256]{1,0:T(8,128)}, f32[2048,256]{1,0:T(8,128)}, f32[2048,256]{1,0:T(8,128)}, f32[2048,256]{1,0:T(8,128)}, f32[256,256]{1,0:T(8,128)}) custom-call(f32[2048,256]{1,0:T(8,128)S(1)} %get-tuple-element.17.refs_0_, f32[2048,256]{1,0:T(8,128)S(1)} %get-tuple-element.18.refs_1_, f32[2048,256]{1,0:T(8,128)S(1)} %get-tuple-element.19.refs_2_, ...), custom_call_target="tpu_custom_call" | custom-call | tf_op jit(solution)/shard_map/pallas_call | solution.py:340
